TPU v7x, 128 devices: a whole 4x4x4 slice. The times are simulated.
128 devices in a mesh: sx: 16 (over x, y_lo, core), sy: 8 (over z, y_hi).
Axes of the slice: x: 4, y: 4 (y_hi: 2, y_lo: 2; y = y_hi * 2 + y_lo), z: 4, core: 2. Of those that a mesh axis runs over, the one named last changes fastest.
Arguments:
- queries: bfloat16 [8192, 128, 128], P(('sx', 'sy')), may hold values from -8 to 8
- keys: bfloat16 [8192, 8, 128], P(('sx', 'sy')), may hold values from -8 to 8
- values: bfloat16 [8192, 8, 128], P(('sx', 'sy')), may hold values from -6 to 6
Outputs:
- attention: bfloat16 [8192, 128, 128], P(('sx', 'sy'))
All inputs are finite; a program needn't handle non-finite values.
Results may differ from a plain program's by a relative error of at most 0.005.
Values may be sent and summed in bfloat16 or wider, within the bound.
A program may use at most 64 MiB of HBM per device.

v0:
```python
import math
import jax
import jax.numpy as jnp
from jax import lax
from jax.sharding import PartitionSpec as P


def frequencies(head_width):
    half_index = jnp.arange(head_width // 2, dtype=jnp.float32)
    base_rate = jnp.power(jnp.float32(500000.0), -2.0 * half_index / head_width)
    wavelen = 2.0 * math.pi / base_rate
    smooth = (8192.0 / wavelen - 1.0) / 3.0
    blended = (1.0 - smooth) * base_rate / 8.0 + smooth * base_rate
    return jnp.where(
        wavelen < 2048.0, base_rate, jnp.where(wavelen > 8192.0, base_rate / 8.0, blended)
    )


def rotate(heads_in, positions):
    head_width = heads_in.shape[-1]
    half_width = head_width // 2
    angles = positions.astype(jnp.float32)[:, None] * frequencies(head_width)[None, :]
    cosine = jnp.cos(angles)[:, None, :]
    sine_wave = jnp.sin(angles)[:, None, :]
    widened = heads_in.astype(jnp.float32)
    front = widened[..., :half_width]
    second = widened[..., half_width:]
    turned = jnp.concatenate(
        [front * cosine - second * sine_wave, second * cosine + front * sine_wave], axis=-1
    )
    return turned.astype(jnp.bfloat16)


def attend(query_matrix, block_rows):
    total_rows, head_width = query_matrix.shape
    score_scale = 1.0 / math.sqrt(head_width)
    query_blocks = total_rows // block_rows
    offsets = jnp.arange(block_rows, dtype=jnp.int32)

    def absorb(running, gathered, start_row):
        key_piece = gathered[0][:, 0]
        value_piece = gathered[1][:, 0]
        pieces = key_piece.shape[0] // block_rows
        key_blocks = key_piece.reshape(pieces, block_rows, head_width)
        value_blocks = value_piece.reshape(pieces, block_rows, head_width)
        first_block = start_row // block_rows

        def per_query(query_index, state_now):
            row_max, row_mass, summed = state_now
            row_start = query_index * block_rows
            query_block = lax.dynamic_slice_in_dim(query_matrix, row_start, block_rows, 0)
            query_places = row_start + offsets

            def per_key(key_step, inner_state):
                block_max, block_mass, block_sum = inner_state
                key_block = lax.dynamic_index_in_dim(key_blocks, key_step, 0, keepdims=False)
                value_block = lax.dynamic_index_in_dim(value_blocks, key_step, 0, keepdims=False)
                key_places = start_row + key_step * block_rows + offsets
                scores = (
                    jnp.dot(query_block, key_block.T, preferred_element_type=jnp.float32)
                    * score_scale
                )
                scores = jnp.where(key_places[None, :] <= query_places[:, None], scores, -jnp.inf)
                new_max = jnp.maximum(block_max, jnp.max(scores, axis=1))
                shrink = jnp.exp(block_max - new_max)
                weights = jnp.exp(scores - new_max[:, None])
                block_mass = block_mass * shrink + jnp.sum(weights, axis=1)
                block_sum = block_sum * shrink[:, None] + jnp.dot(
                    weights.astype(jnp.bfloat16), value_block, preferred_element_type=jnp.float32
                )
                return (new_max, block_mass, block_sum)

            key_count = jnp.clip(query_index - first_block + 1, 0, pieces)
            inner_state = (
                lax.dynamic_slice_in_dim(row_max, row_start, block_rows, 0),
                lax.dynamic_slice_in_dim(row_mass, row_start, block_rows, 0),
                lax.dynamic_slice_in_dim(summed, row_start, block_rows, 0),
            )
            block_max, block_mass, block_sum = lax.fori_loop(0, key_count, per_key, inner_state)
            return (
                lax.dynamic_update_slice_in_dim(row_max, block_max, row_start, 0),
                lax.dynamic_update_slice_in_dim(row_mass, block_mass, row_start, 0),
                lax.dynamic_update_slice_in_dim(summed, block_sum, row_start, 0),
            )

        return lax.fori_loop(0, query_blocks, per_query, running)

    return absorb


def shards(queries, keys, values):
    local_rows, heads_all, head_width = queries.shape
    key_heads = keys.shape[1]
    group_size = heads_all // key_heads
    start_row = lax.axis_index(("sx", "sy")) * local_rows
    positions = start_row + jnp.arange(local_rows, dtype=jnp.int32)
    query_rot = rotate(queries, positions)
    key_rot = rotate(keys, positions)
    ordered = (
        query_rot.reshape(local_rows, key_heads, group_size, head_width)
        .transpose(0, 2, 1, 3)
        .reshape(local_rows, heads_all, head_width)
    )
    query_head = lax.all_to_all(ordered, ("sx", "sy"), split_axis=1, concat_axis=0, tiled=True)
    query_matrix = query_head[:, 0]
    block_rows = local_rows * lax.axis_size("sy")
    total_rows = query_matrix.shape[0]
    absorb = attend(query_matrix, block_rows)
    running = (
        jnp.full((total_rows,), -jnp.inf, jnp.float32),
        jnp.zeros((total_rows,), jnp.float32),
        jnp.zeros((total_rows, head_width), jnp.float32),
    )

    def spread(source):
        widened = jnp.broadcast_to(source[:, None], (local_rows, group_size, key_heads, head_width))
        return widened.reshape(local_rows, heads_all, head_width)

    all_keys, all_values = (
        lax.all_to_all(spread(key_rot), ("sx", "sy"), split_axis=1, concat_axis=0, tiled=True),
        lax.all_to_all(spread(values), ("sx", "sy"), split_axis=1, concat_axis=0, tiled=True),
    )
    running = absorb(running, (all_keys, all_values), jnp.zeros((), jnp.int32))
    row_max, row_mass, summed = running
    result = (summed / row_mass[:, None]).astype(jnp.bfloat16)[:, None, :]
    returned = lax.all_to_all(result, ("sx", "sy"), split_axis=0, concat_axis=1, tiled=True)
    attention = (
        returned.reshape(local_rows, group_size, key_heads, head_width)
        .transpose(0, 2, 1, 3)
        .reshape(local_rows, heads_all, head_width)
    )
    return attention


def solution(mesh):
    placed = (P(("sx", "sy"), None, None), P(("sx", "sy"), None, None), P(("sx", "sy"), None, None))
    return jax.shard_map(
        shards, mesh=mesh, in_specs=placed, out_specs=P(("sx", "sy"), None, None), check_vma=False
    )
```

profile of v0, /device:TPU:1, one launch (start us, length us, event | category | flops | bytes accessed | tf_op | source)
XLA Modules:
  0.0 496.9 jit_solution(14280930461415902531)
XLA Ops:
  0.0 4.1 convert_element_type.27
  4.3 5.0 %subtract_convert_fusion = (bf16[64,128,64]{2,1,0:T(8,128)(2,1)S(1)}, bf16[64,128,64]{2,1,0:T(8,128)(2,1)S(1)}) fusion(f32[64,128,128]{2,1,0:T(8,128)} %convert_element_type.27, f32[64,64]{1,0:T(8,128)S(1)} %get-tuple-element.329, f32[64,64]{1,0:T(8,128)S(1)} %get-tuple-element.328), kind=kLoop, calls=%fused_computation.24 | loop fusion | flops 4194304 | bytes 6324224 | tf_op jit(solution)/shard_map/convert.5
  10.5 2.7 copy.20
  13.1 11.5 %all-to-all-start = ((bf16[64,128,128]{2,0,1:T(8,128)(2,1)}), bf16[64,128,128]{2,0,1:T(8,128)(2,1)S(1)}, u32[]{:S(2)}, u32[]{:S(2)}) async-start(bf16[64,128,128]{2,0,1:T(8,128)(2,1)} %bitcast.6), calls=%async_computation | async-start | bytes 4194304 | tf_op jit(solution)/shard_map/all_to_all | solution.py:104
  25.0 30.1 %all-to-all-done = bf16[64,128,128]{2,0,1:T(8,128)(2,1)S(1)} async-done(((bf16[64,128,128]{2,0,1:T(8,128)(2,1)}), bf16[64,128,128]{2,0,1:T(8,128)(2,1)S(1)}, u32[]{:S(2)}, u32[]{:S(2)}) %all-to-all-start) | async-done | bytes 2097184 | tf_op jit(solution)/shard_map/all_to_all | solution.py:104
  57.1 4.8 all-to-all-start.1
  62.0 29.8 %all-to-all-done.1 = bf16[64,128,128]{2,0,1:T(8,128)(2,1)} async-done(((bf16[64,128,128]{2,0,1:T(8,128)(2,1)}), bf16[64,128,128]{2,0,1:T(8,128)(2,1)}, u32[]{:S(2)}, u32[]{:S(2)}) %all-to-all-start.1) | async-done | bytes 2097184 | tf_op jit(solution)/shard_map/all_to_all | solution.py:120
  93.7 3.9 all-to-all-start.2
  97.6 30.5 %all-to-all-done.2 = bf16[64,128,128]{2,0,1:T(8,128)(2,1)S(1)} async-done(((bf16[64,128,128]{2,0,1:T(8,128)(2,1)}), bf16[64,128,128]{2,0,1:T(8,128)(2,1)S(1)}, u32[]{:S(2)}, u32[]{:S(2)}) %all-to-all-start.2) | async-done | bytes 2097184 | tf_op jit(solution)/shard_map/all_to_all | solution.py:121
  130.3 310.3 %while.67 = (s32[]{:T(128)}, f32[8192]{0:T(1024)S(1)}, f32[8192]{0:T(1024)S(1)}, f32[8192,128]{1,0:T(8,128)}, bf16[8192,128]{1,0:T(8,128)(2,1)}, /*index=5*/bf16...) while((s32[]{:T(128)}, f32[8192]{0:T(1024)S(1)}, ...), condition=%wide.region_5.6_spmd.clone.clone, body=%wide.region_0.5_spmd.clone.clone.sunk | while | flops 136448000 | bytes 5435970 | solution.py:86
  137.6 3.8 while.68
  144.7 5.7 %while.68 = (s32[]{:T(128)}, f32[512]{0:T(512)S(1)}, f32[512]{0:T(512)S(1)}, f32[512,128]{1,0:T(8,128)S(1)}, s32[]{:T(128)}, /*index=5*/s32[512]{0:T(512)S(1)}, ...) while((s32[]{:T(128)}, f32[512]{0:T(512)S(1)}, ...), condition=%wide.region_4.4_spmd, body=%wide.region_1.3_spmd.sunk | while | flops 136447488 | bytes 4104391 | solution.py:79
  153.7 7.6 %while.68 = (s32[]{:T(128)}, f32[512]{0:T(512)S(1)}, f32[512]{0:T(512)S(1)}, f32[512,128]{1,0:T(8,128)S(1)}, s32[]{:T(128)}, /*index=5*/s32[512]{0:T(512)S(1)}, ...) while((s32[]{:T(128)}, f32[512]{0:T(512)S(1)}, ...), condition=%wide.region_4.4_spmd, body=%wide.region_1.3_spmd.sunk | while | flops 136447488 | bytes 4104391 | solution.py:79
  164.6 9.5 %while.68 = (s32[]{:T(128)}, f32[512]{0:T(512)S(1)}, f32[512]{0:T(512)S(1)}, f32[512,128]{1,0:T(8,128)S(1)}, s32[]{:T(128)}, /*index=5*/s32[512]{0:T(512)S(1)}, ...) while((s32[]{:T(128)}, f32[512]{0:T(512)S(1)}, ...), condition=%wide.region_4.4_spmd, body=%wide.region_1.3_spmd.sunk | while | flops 136447488 | bytes 4104391 | solution.py:79
  177.4 11.4 %while.68 = (s32[]{:T(128)}, f32[512]{0:T(512)S(1)}, f32[512]{0:T(512)S(1)}, f32[512,128]{1,0:T(8,128)S(1)}, s32[]{:T(128)}, /*index=5*/s32[512]{0:T(512)S(1)}, ...) while((s32[]{:T(128)}, f32[512]{0:T(512)S(1)}, ...), condition=%wide.region_4.4_spmd, body=%wide.region_1.3_spmd.sunk | while | flops 136447488 | bytes 4104391 | solution.py:79
  192.1 13.2 %while.68 = (s32[]{:T(128)}, f32[512]{0:T(512)S(1)}, f32[512]{0:T(512)S(1)}, f32[512,128]{1,0:T(8,128)S(1)}, s32[]{:T(128)}, /*index=5*/s32[512]{0:T(512)S(1)}, ...) while((s32[]{:T(128)}, f32[512]{0:T(512)S(1)}, ...), condition=%wide.region_4.4_spmd, body=%wide.region_1.3_spmd.sunk | while | flops 136447488 | bytes 4104391 | solution.py:79
  208.7 15.1 %while.68 = (s32[]{:T(128)}, f32[512]{0:T(512)S(1)}, f32[512]{0:T(512)S(1)}, f32[512,128]{1,0:T(8,128)S(1)}, s32[]{:T(128)}, /*index=5*/s32[512]{0:T(512)S(1)}, ...) while((s32[]{:T(128)}, f32[512]{0:T(512)S(1)}, ...), condition=%wide.region_4.4_spmd, body=%wide.region_1.3_spmd.sunk | while | flops 136447488 | bytes 4104391 | solution.py:79
  227.1 17.0 %while.68 = (s32[]{:T(128)}, f32[512]{0:T(512)S(1)}, f32[512]{0:T(512)S(1)}, f32[512,128]{1,0:T(8,128)S(1)}, s32[]{:T(128)}, /*index=5*/s32[512]{0:T(512)S(1)}, ...) while((s32[]{:T(128)}, f32[512]{0:T(512)S(1)}, ...), condition=%wide.region_4.4_spmd, body=%wide.region_1.3_spmd.sunk | while | flops 136447488 | bytes 4104391 | solution.py:79
  247.5 18.9 %while.68 = (s32[]{:T(128)}, f32[512]{0:T(512)S(1)}, f32[512]{0:T(512)S(1)}, f32[512,128]{1,0:T(8,128)S(1)}, s32[]{:T(128)}, /*index=5*/s32[512]{0:T(512)S(1)}, ...) while((s32[]{:T(128)}, f32[512]{0:T(512)S(1)}, ...), condition=%wide.region_4.4_spmd, body=%wide.region_1.3_spmd.sunk | while | flops 136447488 | bytes 4104391 | solution.py:79
  269.7 20.8 %while.68 = (s32[]{:T(128)}, f32[512]{0:T(512)S(1)}, f32[512]{0:T(512)S(1)}, f32[512,128]{1,0:T(8,128)S(1)}, s32[]{:T(128)}, /*index=5*/s32[512]{0:T(512)S(1)}, ...) while((s32[]{:T(128)}, f32[512]{0:T(512)S(1)}, ...), condition=%wide.region_4.4_spmd, body=%wide.region_1.3_spmd.sunk | while | flops 136447488 | bytes 4104391 | solution.py:79
  293.8 22.7 %while.68 = (s32[]{:T(128)}, f32[512]{0:T(512)S(1)}, f32[512]{0:T(512)S(1)}, f32[512,128]{1,0:T(8,128)S(1)}, s32[]{:T(128)}, /*index=5*/s32[512]{0:T(512)S(1)}, ...) while((s32[]{:T(128)}, f32[512]{0:T(512)S(1)}, ...), condition=%wide.region_4.4_spmd, body=%wide.region_1.3_spmd.sunk | while | flops 136447488 | bytes 4104391 | solution.py:79
  319.9 24.6 %while.68 = (s32[]{:T(128)}, f32[512]{0:T(512)S(1)}, f32[512]{0:T(512)S(1)}, f32[512,128]{1,0:T(8,128)S(1)}, s32[]{:T(128)}, /*index=5*/s32[512]{0:T(512)S(1)}, ...) while((s32[]{:T(128)}, f32[512]{0:T(512)S(1)}, ...), condition=%wide.region_4.4_spmd, body=%wide.region_1.3_spmd.sunk | while | flops 136447488 | bytes 4104391 | solution.py:79
  347.8 26.5 %while.68 = (s32[]{:T(128)}, f32[512]{0:T(512)S(1)}, f32[512]{0:T(512)S(1)}, f32[512,128]{1,0:T(8,128)S(1)}, s32[]{:T(128)}, /*index=5*/s32[512]{0:T(512)S(1)}, ...) while((s32[]{:T(128)}, f32[512]{0:T(512)S(1)}, ...), condition=%wide.region_4.4_spmd, body=%wide.region_1.3_spmd.sunk | while | flops 136447488 | bytes 4104391 | solution.py:79
  377.6 28.4 %while.68 = (s32[]{:T(128)}, f32[512]{0:T(512)S(1)}, f32[512]{0:T(512)S(1)}, f32[512,128]{1,0:T(8,128)S(1)}, s32[]{:T(128)}, /*index=5*/s32[512]{0:T(512)S(1)}, ...) while((s32[]{:T(128)}, f32[512]{0:T(512)S(1)}, ...), condition=%wide.region_4.4_spmd, body=%wide.region_1.3_spmd.sunk | while | flops 136447488 | bytes 4104391 | solution.py:79
  409.2 30.2 %while.68 = (s32[]{:T(128)}, f32[512]{0:T(512)S(1)}, f32[512]{0:T(512)S(1)}, f32[512,128]{1,0:T(8,128)S(1)}, s32[]{:T(128)}, /*index=5*/s32[512]{0:T(512)S(1)}, ...) while((s32[]{:T(128)}, f32[512]{0:T(512)S(1)}, ...), condition=%wide.region_4.4_spmd, body=%wide.region_1.3_spmd.sunk | while | flops 136447488 | bytes 4104391 | solution.py:79
  440.6 2.9 fusion.14
  444.0 2.8 reduce
  446.8 3.9 reshape.125
  450.7 34.4 %all_to_all.60 = bf16[128,2,4096]{2,1,0:T(2,128)(2,1)S(1)} all-to-all(bf16[128,2,4096]{2,1,0:T(2,128)(2,1)} %reshape.125), channel_id=1, replica_groups=mesh['sx'=16,'sy'=8] {'sx','sy'}, dimensions={0} | all-to-all | bytes 4194304 | tf_op jit(solution)/shard_map/all_to_all | solution.py:126
  485.1 6.7 %reshape.126 = bf16[8192,1,128]{2,1,0:T(2,128)(2,1)} reshape(bf16[128,2,4096]{2,1,0:T(2,128)(2,1)S(1)} %all_to_all.60) | data formatting | bytes 4194304
  491.8 2.5 copy.27
  494.3 2.7 copy.25
  (1118 shorter events, 313.8 us)
Async XLA Ops:
  13.1 11.5 %copy-start.1 = (bf16[64,8,128]{2,1,0:T(8,128)(2,1)S(1)}, bf16[64,8,128]{2,1,0:T(8,128)(2,1)}, u32[]{:S(2)}) copy-start(bf16[64,8,128]{2,1,0:T(8,128)(2,1)} %param.8) | copy-start | bytes 393220
  13.1 42.0 %all-to-all-start = ((bf16[64,128,128]{2,0,1:T(8,128)(2,1)}), bf16[64,128,128]{2,0,1:T(8,128)(2,1)S(1)}, u32[]{:S(2)}, u32[]{:S(2)}) async-start(bf16[64,128,128]{2,0,1:T(8,128)(2,1)} %bitcast.6), calls=%async_computation | async-start | bytes 4194304 | tf_op jit(solution)/shard_map/all_to_all | solution.py:104
  55.1 2.0 copy-start
  57.1 4.9 copy-start.2
  57.1 34.7 %all-to-all-start.1 = ((bf16[64,128,128]{2,0,1:T(8,128)(2,1)}), bf16[64,128,128]{2,0,1:T(8,128)(2,1)}, u32[]{:S(2)}, u32[]{:S(2)}) async-start(bf16[64,128,128]{2,0,1:T(8,128)(2,1)} %bitcast.10), calls=%async_computation.1 | async-start | bytes 4194304 | tf_op jit(solution)/shard_map/all_to_all | solution.py:120
  93.7 34.4 %all-to-all-start.2 = ((bf16[64,128,128]{2,0,1:T(8,128)(2,1)}), bf16[64,128,128]{2,0,1:T(8,128)(2,1)S(1)}, u32[]{:S(2)}, u32[]{:S(2)}) async-start(bf16[64,128,128]{2,0,1:T(8,128)(2,1)} %bitcast.53), calls=%async_computation.2 | async-start | bytes 4194304 | tf_op jit(solution)/shard_map/all_to_all | solution.py:121
where the time goes:
time: 501 us; the launch traced here: 497 us
  matrix products  221 us (44%)
  waiting for transfers between devices  90.4 us (18%)
  local copies, waits for them, and re-layouts  77.7 us (16%)
  other arithmetic  46.4 us (9%)
  blocking collectives  34.4 us (7%)
  starting transfers between devices  20.3 us (4%)
  loops' own time  6.72 us (1%)
    dot_general x136, matrix products, per_key(): jnp.dot(query_block, key_block.T, preferred_element_type=jnp.float32)  167 us
    dot_general x136, matrix products, per_key(): jnp.dot(weights.astype(jnp.bfloat16), value_block, preferred_element_type...  53.9 us
    all_to_all x1, blocking collectives, shards(): lax.all_to_all(result, ('sx', 'sy'), split_axis=0, concat_axis=1, tiled=T...  34.4 us
    all_to_all x1, waiting for transfers between devices, shards(): lax.all_to_all(spread(values), ('sx', 'sy'), split_axis=1, concat_axis=0,...  30.5 us
    all_to_all x1, waiting for transfers between devices, shards(): lax.all_to_all(ordered, ('sx', 'sy'), split_axis=1, concat_axis=0, tiled=...  30.1 us
    all_to_all x1, waiting for transfers between devices, shards(): lax.all_to_all(spread(key_rot), ('sx', 'sy'), split_axis=1, concat_axis=0...  29.8 us
    reduce_sum x136, other arithmetic, per_key(): block_mass = block_mass * shrink + jnp.sum(weights, axis=1)  26.7 us
    dynamic_slice x16, local copies, waits for them, and re-layouts, per_query(): lax.dynamic_slice_in_dim(summed, row_start, block_rows, 0)  15.5 us
  transfers between devices with their start and end apart: 3, of which 3 were waited for; matrix products, arithmetic and copies ran while one was open for 0% of the time, Pallas kernels for 0%

commit v1 on v0

--- a/solution.py
+++ b/solution.py
@@ -123,7 +123,10 @@
     running = absorb(running, (all_keys, all_values), jnp.zeros((), jnp.int32))
     row_max, row_mass, summed = running
     result = (summed / row_mass[:, None]).astype(jnp.bfloat16)[:, None, :]
-    returned = lax.all_to_all(result, ("sx", "sy"), split_axis=0, concat_axis=1, tiled=True)
+    peers = lax.axis_size(("sx", "sy"))
+    blocks = jnp.stack(jnp.split(result, peers, axis=0), axis=0)
+    blocks = lax.all_to_all(blocks, ("sx", "sy"), split_axis=0, concat_axis=0)
+    returned = jnp.concatenate(blocks, axis=1)
     attention = (
         returned.reshape(local_rows, group_size, key_heads, head_width)
         .transpose(0, 2, 1, 3)

time: 501 us -> 474 us (0.946)
  local copies, waits for them, and re-layouts: 77.7 us -> 65.5 us
  other arithmetic: 46.4 us -> 39 us
  waiting for transfers between devices: 90.4 us -> 83.2 us
    unnamed x10 -> x132, local copies, waits for them, and re-layouts: 13.1 us -> 1.22 us
    all_to_all x1, waiting for transfers between devices: 30.5 us -> 23 us  [shards(): lax.all_to_all(spread(values), ('sx', 'sy'), split_axis=1, concat_axis=0,...]
    all_to_all x1, starting transfers between devices: 11.5 us -> 4.71 us  [shards(): lax.all_to_all(ordered, ('sx', 'sy'), split_axis=1, concat_axis=0, tiled=...]
    all_to_all x1, starting transfers between devices: 4.84 us -> 11.5 us  [shards(): lax.all_to_all(spread(key_rot), ('sx', 'sy'), split_axis=1, concat_axis=0...]
    broadcast_in_dim x2 -> x0, other arithmetic: 5.66 us -> none  [shards(): result = (summed / row_mass[:, None]).astype(jnp.bfloat16)[:, None, :]]
  transfers between devices with their start and end apart: 3 -> 3, of which waited for: 3 -> 3; matrix products, arithmetic and copies ran while one was open for 0% -> 2% of each run, Pallas kernels for 0% -> 0%
where the time goes in v1:
time: 474 us; the launch traced here: 471 us
  matrix products  220 us (46%)
  waiting for transfers between devices  83.2 us (18%)
  local copies, waits for them, and re-layouts  65.5 us (14%)
  other arithmetic  39 us (8%)
  blocking collectives  34.2 us (7%)
  starting transfers between devices  20.1 us (4%)
  loops' own time  7.39 us (2%)
    dot_general x136, matrix products, per_key(): jnp.dot(query_block, key_block.T, preferred_element_type=jnp.float32)  167 us
    dot_general x136, matrix products, per_key(): jnp.dot(weights.astype(jnp.bfloat16), value_block, preferred_element_type...  53.4 us
    all_to_all x1, blocking collectives, shards(): blocks = lax.all_to_all(blocks, ('sx', 'sy'), split_axis=0, concat_axis=0)  34.2 us
    all_to_all x1, waiting for transfers between devices, shards(): lax.all_to_all(spread(key_rot), ('sx', 'sy'), split_axis=1, concat_axis=0...  30.4 us
    all_to_all x1, waiting for transfers between devices, shards(): lax.all_to_all(ordered, ('sx', 'sy'), split_axis=1, concat_axis=0, tiled=...  29.8 us
    reduce_sum x136, other arithmetic, per_key(): block_mass = block_mass * shrink + jnp.sum(weights, axis=1)  26.7 us
    all_to_all x1, waiting for transfers between devices, shards(): lax.all_to_all(spread(values), ('sx', 'sy'), split_axis=1, concat_axis=0,...  23 us
    dynamic_slice x16, local copies, waits for them, and re-layouts, per_query(): lax.dynamic_slice_in_dim(summed, row_start, block_rows, 0)  15.6 us
  transfers between devices with their start and end apart: 3, of which 3 were waited for; matrix products, arithmetic and copies ran while one was open for 2% of the time, Pallas kernels for 0%

profile of v1, /device:TPU:1, one launch (start us, length us, event | category | flops | bytes accessed | tf_op | source)
XLA Modules:
  0.0 470.5 jit_solution(15310732943058141447)
XLA Ops:
  1.5 1.8 broadcast_in_dim.16
  3.3 11.5 %all-to-all-start.1 = ((bf16[64,128,128]{2,0,1:T(8,128)(2,1)}), bf16[64,128,128]{2,0,1:T(8,128)(2,1)S(1)}, u32[]{:S(2)}, u32[]{:S(2)}) async-start(bf16[64,128,128]{2,0,1:T(8,128)(2,1)} %bitcast.10), calls=%async_computation.1 | async-start | bytes 4194304 | tf_op jit(solution)/shard_map/all_to_all | solution.py:120
  14.9 30.4 %all-to-all-done.1 = bf16[64,128,128]{2,0,1:T(8,128)(2,1)S(1)} async-done(((bf16[64,128,128]{2,0,1:T(8,128)(2,1)}), bf16[64,128,128]{2,0,1:T(8,128)(2,1)S(1)}, u32[]{:S(2)}, u32[]{:S(2)}) %all-to-all-start.1) | async-done | bytes 2097184 | tf_op jit(solution)/shard_map/all_to_all | solution.py:120
  45.3 2.0 broadcast_in_dim.17
  47.3 3.9 all-to-all-start.2
  51.2 2.1 convert_element_type.27
  53.3 1.5 subtract_convert_fusion
  56.0 2.7 copy.4
  58.7 23.0 %all-to-all-done.2 = bf16[64,128,128]{2,0,1:T(8,128)(2,1)S(1)} async-done(((bf16[64,128,128]{2,0,1:T(8,128)(2,1)}), bf16[64,128,128]{2,0,1:T(8,128)(2,1)S(1)}, u32[]{:S(2)}, u32[]{:S(2)}) %all-to-all-start.2) | async-done | bytes 2097184 | tf_op jit(solution)/shard_map/all_to_all | solution.py:121
  81.7 4.7 %all-to-all-start = ((bf16[64,128,128]{2,0,1:T(8,128)(2,1)}), bf16[64,128,128]{2,0,1:T(8,128)(2,1)}, u32[]{:S(2)}, u32[]{:S(2)}) async-start(bf16[64,128,128]{2,0,1:T(8,128)(2,1)} %bitcast.561), calls=%async_computation | async-start | bytes 4194304 | tf_op jit(solution)/shard_map/all_to_all | solution.py:104
  86.4 29.8 %all-to-all-done = bf16[64,128,128]{2,0,1:T(8,128)(2,1)} async-done(((bf16[64,128,128]{2,0,1:T(8,128)(2,1)}), bf16[64,128,128]{2,0,1:T(8,128)(2,1)}, u32[]{:S(2)}, u32[]{:S(2)}) %all-to-all-start) | async-done | bytes 2097184 | tf_op jit(solution)/shard_map/all_to_all | solution.py:104
  116.2 2.2 broadcast_in_dim.15
  118.4 310.7 %while.67 = (s32[]{:T(128)}, f32[8192]{0:T(1024)S(1)}, f32[8192]{0:T(1024)S(1)}, f32[8192,128]{1,0:T(8,128)}, bf16[8192,128]{1,0:T(8,128)(2,1)}, /*index=5*/bf16...) while((s32[]{:T(128)}, f32[8192]{0:T(1024)S(1)}, ...), condition=%wide.region_5.6_spmd.clone.clone, body=%wide.region_0.5_spmd.clone.clone.sunk | while | flops 136448000 | bytes 5435962 | solution.py:86
  120.5 1.9 while.68
  125.7 3.8 while.68
  132.8 5.7 %while.68 = (s32[]{:T(128)}, f32[512]{0:T(512)S(1)}, f32[512]{0:T(512)S(1)}, f32[512,128]{1,0:T(8,128)S(1)}, s32[]{:T(128)}, /*index=5*/s32[512]{0:T(512)S(1)}, ...) while((s32[]{:T(128)}, f32[512]{0:T(512)S(1)}, ...), condition=%wide.region_4.4_spmd, body=%wide.region_1.3_spmd.sunk | while | flops 136447488 | bytes 4104391 | solution.py:79
  141.8 7.6 %while.68 = (s32[]{:T(128)}, f32[512]{0:T(512)S(1)}, f32[512]{0:T(512)S(1)}, f32[512,128]{1,0:T(8,128)S(1)}, s32[]{:T(128)}, /*index=5*/s32[512]{0:T(512)S(1)}, ...) while((s32[]{:T(128)}, f32[512]{0:T(512)S(1)}, ...), condition=%wide.region_4.4_spmd, body=%wide.region_1.3_spmd.sunk | while | flops 136447488 | bytes 4104391 | solution.py:79
  152.7 9.5 %while.68 = (s32[]{:T(128)}, f32[512]{0:T(512)S(1)}, f32[512]{0:T(512)S(1)}, f32[512,128]{1,0:T(8,128)S(1)}, s32[]{:T(128)}, /*index=5*/s32[512]{0:T(512)S(1)}, ...) while((s32[]{:T(128)}, f32[512]{0:T(512)S(1)}, ...), condition=%wide.region_4.4_spmd, body=%wide.region_1.3_spmd.sunk | while | flops 136447488 | bytes 4104391 | solution.py:79
  165.5 11.4 %while.68 = (s32[]{:T(128)}, f32[512]{0:T(512)S(1)}, f32[512]{0:T(512)S(1)}, f32[512,128]{1,0:T(8,128)S(1)}, s32[]{:T(128)}, /*index=5*/s32[512]{0:T(512)S(1)}, ...) while((s32[]{:T(128)}, f32[512]{0:T(512)S(1)}, ...), condition=%wide.region_4.4_spmd, body=%wide.region_1.3_spmd.sunk | while | flops 136447488 | bytes 4104391 | solution.py:79
  180.2 13.3 %while.68 = (s32[]{:T(128)}, f32[512]{0:T(512)S(1)}, f32[512]{0:T(512)S(1)}, f32[512,128]{1,0:T(8,128)S(1)}, s32[]{:T(128)}, /*index=5*/s32[512]{0:T(512)S(1)}, ...) while((s32[]{:T(128)}, f32[512]{0:T(512)S(1)}, ...), condition=%wide.region_4.4_spmd, body=%wide.region_1.3_spmd.sunk | while | flops 136447488 | bytes 4104391 | solution.py:79
  196.8 15.2 %while.68 = (s32[]{:T(128)}, f32[512]{0:T(512)S(1)}, f32[512]{0:T(512)S(1)}, f32[512,128]{1,0:T(8,128)S(1)}, s32[]{:T(128)}, /*index=5*/s32[512]{0:T(512)S(1)}, ...) while((s32[]{:T(128)}, f32[512]{0:T(512)S(1)}, ...), condition=%wide.region_4.4_spmd, body=%wide.region_1.3_spmd.sunk | while | flops 136447488 | bytes 4104391 | solution.py:79
  215.3 17.1 %while.68 = (s32[]{:T(128)}, f32[512]{0:T(512)S(1)}, f32[512]{0:T(512)S(1)}, f32[512,128]{1,0:T(8,128)S(1)}, s32[]{:T(128)}, /*index=5*/s32[512]{0:T(512)S(1)}, ...) while((s32[]{:T(128)}, f32[512]{0:T(512)S(1)}, ...), condition=%wide.region_4.4_spmd, body=%wide.region_1.3_spmd.sunk | while | flops 136447488 | bytes 4104391 | solution.py:79
  235.6 19.0 %while.68 = (s32[]{:T(128)}, f32[512]{0:T(512)S(1)}, f32[512]{0:T(512)S(1)}, f32[512,128]{1,0:T(8,128)S(1)}, s32[]{:T(128)}, /*index=5*/s32[512]{0:T(512)S(1)}, ...) while((s32[]{:T(128)}, f32[512]{0:T(512)S(1)}, ...), condition=%wide.region_4.4_spmd, body=%wide.region_1.3_spmd.sunk | while | flops 136447488 | bytes 4104391 | solution.py:79
  257.9 20.9 %while.68 = (s32[]{:T(128)}, f32[512]{0:T(512)S(1)}, f32[512]{0:T(512)S(1)}, f32[512,128]{1,0:T(8,128)S(1)}, s32[]{:T(128)}, /*index=5*/s32[512]{0:T(512)S(1)}, ...) while((s32[]{:T(128)}, f32[512]{0:T(512)S(1)}, ...), condition=%wide.region_4.4_spmd, body=%wide.region_1.3_spmd.sunk | while | flops 136447488 | bytes 4104391 | solution.py:79
  282.1 22.8 %while.68 = (s32[]{:T(128)}, f32[512]{0:T(512)S(1)}, f32[512]{0:T(512)S(1)}, f32[512,128]{1,0:T(8,128)S(1)}, s32[]{:T(128)}, /*index=5*/s32[512]{0:T(512)S(1)}, ...) while((s32[]{:T(128)}, f32[512]{0:T(512)S(1)}, ...), condition=%wide.region_4.4_spmd, body=%wide.region_1.3_spmd.sunk | while | flops 136447488 | bytes 4104391 | solution.py:79
  308.1 24.6 %while.68 = (s32[]{:T(128)}, f32[512]{0:T(512)S(1)}, f32[512]{0:T(512)S(1)}, f32[512,128]{1,0:T(8,128)S(1)}, s32[]{:T(128)}, /*index=5*/s32[512]{0:T(512)S(1)}, ...) while((s32[]{:T(128)}, f32[512]{0:T(512)S(1)}, ...), condition=%wide.region_4.4_spmd, body=%wide.region_1.3_spmd.sunk | while | flops 136447488 | bytes 4104391 | solution.py:79
  336.1 26.5 %while.68 = (s32[]{:T(128)}, f32[512]{0:T(512)S(1)}, f32[512]{0:T(512)S(1)}, f32[512,128]{1,0:T(8,128)S(1)}, s32[]{:T(128)}, /*index=5*/s32[512]{0:T(512)S(1)}, ...) while((s32[]{:T(128)}, f32[512]{0:T(512)S(1)}, ...), condition=%wide.region_4.4_spmd, body=%wide.region_1.3_spmd.sunk | while | flops 136447488 | bytes 4104391 | solution.py:79
  365.9 28.4 %while.68 = (s32[]{:T(128)}, f32[512]{0:T(512)S(1)}, f32[512]{0:T(512)S(1)}, f32[512,128]{1,0:T(8,128)S(1)}, s32[]{:T(128)}, /*index=5*/s32[512]{0:T(512)S(1)}, ...) while((s32[]{:T(128)}, f32[512]{0:T(512)S(1)}, ...), condition=%wide.region_4.4_spmd, body=%wide.region_1.3_spmd.sunk | while | flops 136447488 | bytes 4104391 | solution.py:79
  397.6 30.3 %while.68 = (s32[]{:T(128)}, f32[512]{0:T(512)S(1)}, f32[512]{0:T(512)S(1)}, f32[512,128]{1,0:T(8,128)S(1)}, s32[]{:T(128)}, /*index=5*/s32[512]{0:T(512)S(1)}, ...) while((s32[]{:T(128)}, f32[512]{0:T(512)S(1)}, ...), condition=%wide.region_4.4_spmd, body=%wide.region_1.3_spmd.sunk | while | flops 136447488 | bytes 4104391 | solution.py:79
  429.1 2.9 divide_convert_fusion
  433.7 34.2 %all_to_all.50 = bf16[128,64,1,128]{3,1,2,0:T(8,128)(2,1)S(1)} all-to-all(bf16[128,64,1,128]{3,1,2,0:T(8,128)(2,1)S(1)} %constant_dynamic-update-slice_fusion.1), channel_id=1, replica_groups=mesh['sx'=16,'sy'=8] {'sx','sy'}, dimensions={0} | all-to-all | bytes 4194304 | tf_op jit(solution)/shard_map/all_to_all | solution.py:128
  467.8 2.7 copy.7
  (1239 shorter events, 307.1 us)
Async XLA Ops:
  3.3 11.5 %copy-start.1 = (bf16[64,8,128]{2,1,0:T(8,128)(2,1)S(1)}, bf16[64,8,128]{2,1,0:T(8,128)(2,1)}, u32[]{:S(2)}) copy-start(bf16[64,8,128]{2,1,0:T(8,128)(2,1)} %param.9) | copy-start | bytes 393220
  3.3 42.0 %all-to-all-start.1 = ((bf16[64,128,128]{2,0,1:T(8,128)(2,1)}), bf16[64,128,128]{2,0,1:T(8,128)(2,1)S(1)}, u32[]{:S(2)}, u32[]{:S(2)}) async-start(bf16[64,128,128]{2,0,1:T(8,128)(2,1)} %bitcast.10), calls=%async_computation.1 | async-start | bytes 4194304 | tf_op jit(solution)/shard_map/all_to_all | solution.py:120
  45.3 2.0 copy-start
  47.3 34.4 %all-to-all-start.2 = ((bf16[64,128,128]{2,0,1:T(8,128)(2,1)}), bf16[64,128,128]{2,0,1:T(8,128)(2,1)S(1)}, u32[]{:S(2)}, u32[]{:S(2)}) async-start(bf16[64,128,128]{2,0,1:T(8,128)(2,1)} %bitcast.560), calls=%async_computation.2 | async-start | bytes 4194304 | tf_op jit(solution)/shard_map/all_to_all | solution.py:121
  81.7 34.5 %all-to-all-start = ((bf16[64,128,128]{2,0,1:T(8,128)(2,1)}), bf16[64,128,128]{2,0,1:T(8,128)(2,1)}, u32[]{:S(2)}, u32[]{:S(2)}) async-start(bf16[64,128,128]{2,0,1:T(8,128)(2,1)} %bitcast.561), calls=%async_computation | async-start | bytes 4194304 | tf_op jit(solution)/shard_map/all_to_all | solution.py:104
